TPU v7x, 256 devices: a whole 4x4x8 slice. The times are simulated.
256 devices in a mesh: grp: 8 (over y, core), blk: 32 (over x, z).
Axes of the slice: x: 4, y: 4, z: 8, core: 2. Of those that a mesh axis runs over, the one named last changes fastest.
Arguments:
- node_vars: bfloat16 [112, 98304], P(None, ('grp', 'blk')), may hold values from -6 to 6
- w_in: bfloat16 [512, 112], replicated, may hold values from -0.5 to 0.5
- w_out: bfloat16 [96, 512], replicated, may hold values from -0.25 to 0.25
- linear_part: bfloat16 [96, 112], replicated, may hold values from -0.1875 to 0.1875
- step_len: float32 [512, 8], P(('grp', 'blk')), may hold values from 0.02 to 1.08
- path_count: int32 [512, 8], P(('grp', 'blk')), may hold values from 1 to 16, as said below
- path_node: int32 [512, 8, 16], P(('grp', 'blk')), may hold values from 0 to 23
- path_con: int32 [512, 8, 16], P(('grp', 'blk')), may hold values from 0 to 95
Outputs:
- tangent: bfloat16 [98304, 10752], P(('grp', 'blk'))
- path_rows: bfloat16 [112, 65536], P(None, ('grp', 'blk'))
- row_start: int32 [256], P(('grp', 'blk'))
Inputs may be any that keep to these rules, and one draw needn't show every extreme that they name: `path_count`: the path-constraint rows of one device number at most 256, and in every group one device has exactly that many.
All inputs are finite; a program needn't handle non-finite values.
Results may differ from a plain program's by a relative error of at most 0.0012.
The roundings to bfloat16 on the way count: a program that leaves them out, or rounds other values in their place, can miss the bound.
Values may be sent and summed in bfloat16 or wider, within the bound.
A program may use at most 192 MiB of HBM per device.

v0:
```python
import functools

import jax
import jax.numpy as jnp
from jax import lax
from jax.sharding import Mesh
from jax.sharding import PartitionSpec as P

STATES = 96
UNITS = 512
NODES = 24
MAXP = 16
VARS = 112
BLK = ("blk_0", "blk_1")
GRP_BLK = ("grp_0", "grp_1", "blk_0", "blk_1")
GRP = ("grp_0", "grp_1")


def neutral_like(shard, identity):
    return jnp.zeros_like(shard) + jnp.asarray(identity, shard.dtype)


def carried_in(shard, axes, combine, identity):
    before = start = neutral_like(shard, identity)
    running = shard
    for axis in reversed(axes):
        devices, position = (lax.axis_size(axis), lax.axis_index(axis))
        pieces = lax.all_gather(running, axis)
        inside, running = (start, start)
        for k in range(devices):
            passed = k < position
            running = combine(running, pieces[k])
            inside = jnp.where(passed, running, inside)
        before = combine(inside, before)
    return before


def over_axes(shard, axes):
    return functools.reduce(lax.psum, axes, shard)


def add_ints(earlier, later):
    return earlier + later


def node_blocks(slope_block, w_in, w_out32, linear32):
    scaled = (w_out32[None, :, :] * slope_block[:, None, :]).astype(jnp.bfloat16)
    node_count = scaled.shape[0]
    products = jnp.dot(
        scaled.reshape(node_count * STATES, UNITS), w_in, preferred_element_type=jnp.float32
    )
    return products.reshape(node_count, STATES, VARS) + linear32[None, :, :]


def direct_rows(slopes_t, node_index, con_index, w_in, w_out32, linear32):
    scaled_rows = (w_out32[con_index] * slopes_t[node_index]).astype(jnp.bfloat16)
    return (
        jnp.dot(scaled_rows, w_in, preferred_element_type=jnp.float32) + linear32[con_index]
    ).astype(jnp.bfloat16)


def local(node_vars, w_in, w_out, linear_part, step_len, path_count, path_node, path_con):
    row_count = node_vars.shape[1]
    pair_count = path_count.shape[0] * path_count.shape[1]
    slot_count = pair_count * MAXP
    preact = jnp.dot(w_in, node_vars, preferred_element_type=jnp.float32)
    slopes_t = (1.0 - jnp.tanh(preact) ** 2).T
    w_out32 = w_out.astype(jnp.float32)
    linear32 = linear_part.astype(jnp.float32)
    node_index = (
        jnp.arange(pair_count, dtype=jnp.int32)[:, None] * NODES
        + path_node.reshape(pair_count, MAXP)
    ).reshape(-1)
    con_index = path_con.reshape(-1)
    path_entry = direct_rows(slopes_t, node_index, con_index, w_in, w_out32, linear32)

    def compute_block(slope_block):
        return node_blocks(slope_block, w_in, w_out32, linear32)

    jacobian = lax.map(compute_block, slopes_t.reshape(pair_count, NODES, UNITS)).reshape(
        row_count, STATES, VARS
    )
    counts = path_count.reshape(pair_count)
    own_total = jnp.sum(counts)
    group_offset = carried_in(own_total, BLK, add_ints, jnp.int32(0))
    row_first = carried_in(own_total, GRP_BLK, add_ints, jnp.int32(0))
    earlier = jnp.cumsum(counts) - counts
    slot_index = jnp.arange(MAXP, dtype=jnp.int32)
    live_slot = (slot_index[None, :] < counts[:, None]).reshape(-1)
    target = (group_offset + earlier[:, None] + slot_index[None, :]).reshape(-1).astype(jnp.int32)
    blk_size = lax.axis_size(BLK)
    owners = jnp.where(live_slot, target % blk_size, blk_size)
    within = target // blk_size
    buffer = (
        jnp.zeros((blk_size, VARS, slot_count), jnp.bfloat16)
        .at[owners, :, within]
        .set(path_entry, mode="drop")
    )
    received = lax.all_to_all(buffer, BLK, split_axis=0, concat_axis=0, tiled=True)
    path_rows = jnp.sum(received.astype(jnp.float32), axis=0).astype(jnp.bfloat16)
    half_step = jnp.repeat(step_len.reshape(-1) * 0.5, NODES)
    defect = half_step[:, None, None] * jacobian
    column_sq = over_axes(jnp.sum(defect * defect, axis=(0, 1)), GRP_BLK)
    entry_total = row_count * lax.axis_size(GRP) * blk_size * STATES
    column_norm = jnp.sqrt(column_sq / entry_total + 1e-06)
    tangent = (
        (defect / column_norm[None, None, :]).astype(jnp.bfloat16).reshape(row_count, STATES * VARS)
    )
    return (tangent, path_rows, row_first.reshape(1))


def solution(mesh):
    split = Mesh(mesh.devices.reshape(4, 2, 4, 8), ("grp_0", "grp_1", "blk_0", "blk_1"))
    return jax.shard_map(
        local,
        mesh=split,
        in_specs=(
            P(None, GRP_BLK),
            P(),
            P(),
            P(),
            P(GRP_BLK, None),
            P(GRP_BLK, None),
            P(GRP_BLK, None, None),
            P(GRP_BLK, None, None),
        ),
        out_specs=(P(GRP_BLK, None), P(None, GRP_BLK), P(GRP_BLK)),
        check_vma=False,
    )
```

profile of v0, /device:TPU:8, one launch (start us, length us, event | category | flops | bytes accessed | tf_op | source)
XLA Modules:
  0.0 204.3 jit_solution(8659877599321971559)
XLA Ops:
  0.7 0.8 lt.79
  1.5 0.8 reshape.328
  2.2 0.9 convert_element_type.23
  3.2 1.3 reduce_sum.31
  4.5 1.3 dynamic-slice
  5.8 1.4 dynamic-update-slice
  7.2 0.7 convert_element_type.24
  7.9 16.1 %all-reduce = s32[8]{0:T(128)S(1)} all-reduce(s32[8]{0:T(128)S(1)} %dynamic-update-slice), channel_id=1, replica_groups=mesh['grp_0'=4,'grp_1'=2,'blk_0'=4,'blk_1'=8] {'blk_1'}, use_global_device_ids=true, to_apply=%add | all-reduce | flops 8 | bytes 64
  24.7 1.3 dynamic-slice.1
  31.9 8.9 %all-reduce.1 = s32[4]{0:T(128)S(1)} all-reduce(s32[4]{0:T(128)S(1)} %dynamic-update-slice.1), channel_id=1, replica_groups=mesh['grp_0'=4,'grp_1'=2,'blk_0'=4,'blk_1'=8] {'blk_0'}, use_global_device_ids=true, to_apply=%add.1 | all-reduce | flops 4 | bytes 32
  45.5 0.8 reshape.274
  47.1 1.0 gather_fusion
  48.3 0.8 reshape.275
  49.1 1.2 fusion.8
  50.3 1.0 gather_fusion.1
  51.3 1.1 fusion.9
  53.0 12.6 %scatter_fusion = bf16[32,112,256]{1,2,0:T(8,128)(2,1)S(1)} fusion(bf16[32,112,256]{1,2,0:T(8,128)(2,1)S(1)} %broadcast_in_dim.16, s32[256]{0:T(256)S(1)} %bitcast.52, bf16[256,112]{1,0:T(8,128)(2,1)S(1)} %copy.19), kind=kCustom, calls=%fused_computation.3 | custom fusion | bytes 174080 | tf_op jit(solution)/shard_map/scatter | solution.py:97
  65.6 2.8 %copy.20 = bf16[32,112,256]{2,1,0:T(8,128)(2,1)} copy(bf16[32,112,256]{1,2,0:T(8,128)(2,1)S(1)} %scatter_fusion) | data formatting | bytes 3670016 | tf_op jit(solution)/shard_map/scatter | solution.py:97
  68.5 4.1 %all-to-all-start = ((bf16[32,112,256]{2,1,0:T(8,128)(2,1)}), bf16[32,112,256]{2,1,0:T(8,128)(2,1)S(1)}, u32[]{:S(2)}, u32[]{:S(2)}) async-start(bf16[32,112,256]{2,1,0:T(8,128)(2,1)} %copy.20), calls=%async_computation | async-start | bytes 3670016 | tf_op jit(solution)/shard_map/all_to_all | solution.py:99
  72.6 29.2 %while.10 = (s32[]{:T(128)}, f32[16,24,96,112]{3,2,1,0:T(8,128)}, f32[96,512]{1,0:T(8,128)S(1)}, f32[16,24,512]{2,1,0:T(8,128)S(1)}, bf16[512,112]{0,1:T(8,128)(2,1)S(1)}, /*index=5*/f32[96,112]{1,0:T(8,128)S(1)}, s32[]{:T(128)}) while((s32[]{:T(128)}, f32[16,24,96,112]{3,2,1,0:T(8,128)}, f32[96,512]{1,0:T(8,128)S(1)}, ...), condition=%wide.region_1.2_spmd, body=%wide.region_0.1_spmd.sunk | while | flops 266858496 | bytes 1681501 | solution.py:80
  72.7 1.8 fusion.22
  74.5 1.8 fusion.22
  76.3 1.8 fusion.22
  78.1 1.8 fusion.22
  79.9 1.8 fusion.22
  81.7 1.8 fusion.22
  83.6 1.8 fusion.22
  85.3 1.9 fusion.22
  87.2 1.8 fusion.22
  89.0 1.8 fusion.22
  90.9 1.8 fusion.22
  92.7 1.8 fusion.22
  94.5 1.8 fusion.22
  96.4 1.8 fusion.22
  98.2 1.8 fusion.22
  100.0 1.9 fusion.22
  102.5 0.8 dynamic-update-slice.2
  103.3 1.8 all-reduce.2
  107.6 0.8 dynamic-update-slice.3
  108.4 11.3 %multiply_reduce_fusion = f32[112]{0:T(128)S(1)} fusion(f32[16,24,96,112]{3,2,1,0:T(8,128)} %get-tuple-element.35, f32[16]{0:T(128)S(1)} %mul.55), kind=kLoop, calls=%fused_computation.13 | loop fusion | flops 12386192 | bytes 16515584 | tf_op jit(solution)/shard_map/reduce_sum | solution.py:103
  119.7 8.3 %all-reduce.3 = s32[4]{0:T(128)S(1)} all-reduce(s32[4]{0:T(128)S(1)} %dynamic-update-slice.3), channel_id=1, replica_groups=mesh['grp_0'=4,'grp_1'=2,'blk_0'=4,'blk_1'=8] {'grp_0'}, use_global_device_ids=true, to_apply=%add.3 | all-reduce | flops 4 | bytes 32
  128.0 21.1 %reshape.271 = f32[384,10752]{1,0:T(8,128)} reshape(f32[16,24,96,112]{3,2,1,0:T(8,128)} %get-tuple-element.35) | data formatting | bytes 33030144 | tf_op jit(solution)/shard_map/reshape | solution.py:80
  149.1 8.9 %psum.28 = f32[112]{0:T(128)S(1)} all-reduce(f32[112]{0:T(128)S(1)} %multiply_reduce_fusion), channel_id=1, replica_groups=mesh['grp_0'=4,'grp_1'=2,'blk_0'=4,'blk_1'=8] {'grp_0'}, use_global_device_ids=true, to_apply=%region_3.4 | all-reduce | flops 112 | bytes 896 | tf_op jit(solution)/shard_map/psum | solution.py:39
  158.1 2.5 %psum.29 = f32[112]{0:T(128)S(1)} all-reduce(f32[112]{0:T(128)S(1)} %psum.28), channel_id=1, replica_groups=mesh['grp_0'=4,'grp_1'=2,'blk_0'=4,'blk_1'=8] {'grp_1'}, use_global_device_ids=true, to_apply=%region_4.5 | all-reduce | flops 112 | bytes 896 | tf_op jit(solution)/shard_map/psum | solution.py:39
  160.5 10.8 %psum.30 = f32[112]{0:T(128)S(1)} all-reduce(f32[112]{0:T(128)S(1)} %psum.29), channel_id=1, replica_groups=mesh['grp_0'=4,'grp_1'=2,'blk_0'=4,'blk_1'=8] {'blk_0'}, use_global_device_ids=true, to_apply=%region_5.6 | all-reduce | flops 112 | bytes 896 | tf_op jit(solution)/shard_map/psum | solution.py:39
  171.3 16.9 %psum.31 = f32[112]{0:T(128)S(1)} all-reduce(f32[112]{0:T(128)S(1)} %psum.30), channel_id=1, replica_groups=mesh['grp_0'=4,'grp_1'=2,'blk_0'=4,'blk_1'=8] {'blk_1'}, use_global_device_ids=true, to_apply=%region_6.7 | all-reduce | flops 112 | bytes 896 | tf_op jit(solution)/shard_map/psum | solution.py:39
  193.0 9.2 %divide_convert_fusion = bf16[384,10752]{1,0:T(8,128)(2,1)} fusion(f32[384,10752]{1,0:T(8,128)} %reshape.271, f32[10752]{0:T(1024)S(1)} %div.34, f32[384]{0:T(512)S(1)} %mul.56), kind=kLoop, calls=%fused_computation.14 | loop fusion | flops 12386304 | bytes 24817152 | tf_op jit(solution)/shard_map/convert_element_type | solution.py:107
  202.3 0.9 reduce_sum.32
  (65 shorter events, 6.9 us)
Async XLA Ops:
  0.6 48.4 %copy-start = (bf16[112,384]{1,0:T(8,128)(2,1)S(1)}, bf16[112,384]{1,0:T(8,128)(2,1)}, u32[]{:S(2)}) copy-start(bf16[112,384]{1,0:T(8,128)(2,1)} %param.10) | copy-start | bytes 258052
  0.6 72.0 %copy-start.1 = (bf16[512,112]{0,1:T(8,128)(2,1)S(1)}, bf16[512,112]{0,1:T(8,128)(2,1)}, u32[]{:S(2)}) copy-start(bf16[512,112]{0,1:T(8,128)(2,1)} %param.11) | copy-start | bytes 344068
  50.3 51.6 %copy-start.2 = (f32[2,8]{1,0:T(2,128)S(1)}, f32[2,8]{1,0:T(2,128)}, u32[]{:S(2)}) copy-start(f32[2,8]{1,0:T(2,128)} %param.14) | copy-start | bytes 196
  50.3 51.6 %copy-start.4 = (u32[256]{0:T(256)S(1)}, u32[256]{0:T(256)}, u32[]{:S(2)}) copy-start(u32[256]{0:T(256)} %constant.129) | copy-start | bytes 3076
  50.3 55.4 %copy-start.3 = (u32[256]{0:T(256)S(1)}, u32[256]{0:T(256)}, u32[]{:S(2)}) copy-start(u32[256]{0:T(256)} %constant.134) | copy-start | bytes 3076
  68.5 133.8 %all-to-all-start = ((bf16[32,112,256]{2,1,0:T(8,128)(2,1)}), bf16[32,112,256]{2,1,0:T(8,128)(2,1)S(1)}, u32[]{:S(2)}, u32[]{:S(2)}) async-start(bf16[32,112,256]{2,1,0:T(8,128)(2,1)} %copy.20), calls=%async_computation | async-start | bytes 3670016 | tf_op jit(solution)/shard_map/all_to_all | solution.py:99
where the time goes:
time: 206 us; the launch traced here: 204 us
  blocking collectives  74.2 us (36%)
  local copies, waits for them, and re-layouts  53.6 us (26%)
  matrix products  31.4 us (15%)
  other arithmetic  24.8 us (12%)
  between operations  16.2 us (8%)
  starting transfers between devices  4.13 us (2%)
    psum x4, blocking collectives, over_axes(): return functools.reduce(lax.psum, axes, shard)  39 us
    unnamed x4, blocking collectives  35.1 us
    dot_general x16, matrix products, node_blocks(): jnp.dot(scaled.reshape(node_count * STATES, UNITS), w_in, preferred_eleme...  29.1 us
    reshape x1, local copies, waits for them, and re-layouts, local(): lax.map(compute_block, slopes_t.reshape(pair_count, NODES, UNITS))  21.1 us
    scatter x2, local copies, waits for them, and re-layouts, local(): buffer = jnp.zeros((blk_size, VARS, slot_count), jnp.bfloat16).at[owners,...  15.4 us
    reduce_sum x1, other arithmetic, local(): column_sq = over_axes(jnp.sum(defect * defect, axis=(0, 1)), GRP_BLK)  11.3 us
    convert_element_type x1, other arithmetic, local(): (defect / column_norm[None, None, :]).astype(jnp.bfloat16)  9.24 us
    unnamed x22, local copies, waits for them, and re-layouts  7.39 us
  transfers between devices with their start and end apart: 1, of which 0 were waited for; matrix products, arithmetic and copies ran while one was open for 37% of the time, Pallas kernels for 0%

commit v1 on v0

v1 whole, which is shorter than its diff:
```python
import functools

import jax
import jax.numpy as jnp
from jax import lax
from jax.experimental import pallas as pl
from jax.experimental.pallas import tpu as pltpu
from jax.sharding import PartitionSpec as P

STATES = 96
UNITS = 512
NODES = 24
MAXP = 16
VARS = 112
LANES = 128
GROUP = 8
STEPS = STATES // GROUP
SENT_ROWS = 8
EARLY = 2
MESH = pl.DeviceIdType.MESH
BF16 = jnp.bfloat16
F32 = jnp.float32


def dot(a, b, dims):
    return lax.dot_general(a, b, (dims, ((), ())), preferred_element_type=F32)


def nn(a, b):
    return dot(a, b, ((1,), (0,)))


def nt(a, b):
    return dot(a, b, ((1,), (1,)))


def tn(a, b):
    return dot(a, b, ((0,), (0,)))


def iota(shape, axis):
    return lax.broadcasted_iota(jnp.int32, shape, axis)


def split2(x):
    high = x.astype(BF16)
    return high, (x - high.astype(F32)).astype(BF16)


def split3(x):
    high = x.astype(BF16)
    rest = x - high.astype(F32)
    mid = rest.astype(BF16)
    return high, mid, (rest - mid.astype(F32)).astype(BF16)


def front(
    n_grp, n_blk,
    vars_ref, w_in_t_ref, w_out_ref, linear_ref, step_ref, count_ref, node_ref, con_ref,
    defect_ref, inv_ref, place_ref, rows_ref, start_ref,
    slopes, w_cols, l_cols, half_row, entry, msg1, recv1, msg2, recv2, send_rows, recv_rows,
    s1_send, s1_recv, s2_send, s2_recv, s3_send, s3_recv,
):
    grp, blk = lax.axis_index("grp"), lax.axis_index("blk")
    pairs = count_ref.shape[0] * count_ref.shape[1]
    traj = count_ref.shape[1]
    rows = vars_ref.shape[1]
    slots = pairs * MAXP

    barrier = pltpu.get_barrier_semaphore()

    @pl.loop(1, n_blk)
    def _(i):
        pl.semaphore_signal(barrier, inc=1, device_id={"blk": lax.rem(blk + i, n_blk)}, device_id_type=MESH)

    @pl.loop(1, n_grp)
    def _(i):
        pl.semaphore_signal(barrier, inc=1, device_id={"grp": lax.rem(grp + i, n_grp)}, device_id_type=MESH)

    w_in_t = w_in_t_ref[...]
    w_out = w_out_ref[...]
    linear = linear_ref[...]
    preact = tn(w_in_t, vars_ref[...])
    th = jnp.tanh(preact)
    slopes[...] = 1.0 - th * th

    row_pair = iota((1, rows), 1) // NODES
    half = jnp.zeros((1, rows), F32)
    for e in range(pairs):
        half = jnp.where(row_pair == e, step_ref[e // traj, e % traj] * 0.5, half)
    half_row[...] = half

    scaled = slopes[...] * half
    high, low = split2(scaled)
    gram = nt(high, high) + 2.0 * nt(high, low)
    m_high, m_low = split2(tn(w_out, w_out) * gram)
    w_in = w_in_t.astype(F32).T
    w_in16 = w_in.astype(BF16)
    inner = nn(m_high, w_in16) + nn(m_low, w_in16)
    cross = jnp.sum(scaled * half, axis=1, keepdims=True) * tn(w_out, linear)
    linear32 = linear.astype(F32)
    column = jnp.sum(w_in * (inner + 2.0 * cross), axis=0, keepdims=True)
    column += jnp.sum(half * half) * jnp.sum(linear32 * linear32, axis=0, keepdims=True)

    own_total = jnp.int32(0)
    befores = []
    for e in range(pairs):
        befores.append(own_total)
        own_total += count_ref[e // traj, e % traj]
    tail = jnp.where(iota((1, LANES - VARS), 1) == 0, own_total.astype(F32), 0.0)
    message = jnp.concatenate([column, tail], axis=1)
    msg1[0] = message
    recv1[blk] = message

    w_t = w_out.astype(F32).T
    l_t = linear32.T
    for g in range(STEPS):
        w_cols[g] = w_t[:, g * GROUP:(g + 1) * GROUP]
        l_cols[g] = l_t[:, g * GROUP:(g + 1) * GROUP]

    def main(g):
        for k in range(0, GROUP, 2):
            cols = w_cols[g]
            here = slopes[...]
            block = jnp.concatenate([here * cols[:, k:k + 1], here * cols[:, k + 1:k + 2]], axis=1)
            product = nn(w_in_t, block.astype(BF16))
            lin = l_cols[g]
            for j in range(2):
                part = product[:, j * rows:(j + 1) * rows] + lin[:, k + j:k + j + 1]
                defect_ref[g * GROUP + k + j] = part * half_row[...]

    slot_pair = iota((slots, 1), 0) // MAXP
    slot_k = iota((slots, 1), 0) % MAXP
    count = jnp.zeros((slots, 1), jnp.int32)
    before = jnp.zeros((slots, 1), jnp.int32)
    for e in range(pairs):
        count = jnp.where(slot_pair == e, count_ref[e // traj, e % traj], count)
        before = jnp.where(slot_pair == e, befores[e], before)
    number = jnp.where(slot_k < count, before + slot_k, -1)

    def by_slot(ref):
        table = ref[...].reshape(pairs, 1, MAXP).astype(F32)
        wide = jnp.broadcast_to(table, (pairs, MAXP, MAXP)).reshape(slots, MAXP)
        mine = iota((slots, MAXP), 1) == slot_k
        return jnp.sum(jnp.where(mine, wide, 0.0), axis=1, keepdims=True).astype(jnp.int32)

    node = slot_pair * NODES + by_slot(node_ref)
    con = by_slot(con_ref)
    pick_node = (iota((slots, rows), 1) == node).astype(F32).astype(BF16)
    pick_con = (iota((slots, STATES), 1) == con).astype(F32).astype(BF16)
    s_high, s_mid, s_low = split3(slopes[...])
    slope_rows = nt(pick_node, s_high) + (nt(pick_node, s_mid) + nt(pick_node, s_low))
    scaled_rows = (nn(pick_con, w_out) * slope_rows).astype(BF16)
    entry_rows = nt(scaled_rows, w_in_t) + nn(pick_con, linear)
    entry[...] = jnp.concatenate([entry_rows, jnp.zeros((slots, LANES - VARS), F32)], axis=1).astype(BF16)

    @pl.loop(0, EARLY)
    def _(g):
        main(g)

    pl.semaphore_wait(barrier, n_blk + n_grp - 2)

    def copy1(i):
        peer = lax.rem(blk + i, n_blk)
        return pltpu.make_async_remote_copy(
            src_ref=msg1.at[0], dst_ref=recv1.at[blk], send_sem=s1_send.at[peer], recv_sem=s1_recv.at[blk],
            device_id={"blk": peer}, device_id_type=MESH)

    @pl.loop(1, n_blk)
    def _(i):
        copy1(i).start()

    @pl.loop(EARLY, STEPS)
    def _(g):
        main(g)

    @pl.loop(1, n_blk)
    def _(i):
        peer = lax.rem(blk + i, n_blk)
        pltpu.make_async_remote_copy(
            src_ref=msg1.at[0], dst_ref=recv1.at[peer], send_sem=s1_send.at[peer], recv_sem=s1_recv.at[peer],
            device_id={"blk": peer}, device_id_type=MESH).wait_recv()

    table = recv1[...].reshape(n_blk, LANES)
    message2 = jnp.sum(table, axis=0, keepdims=True)
    msg2[0] = message2
    recv2[grp] = message2

    def copy2(i):
        peer = lax.rem(grp + i, n_grp)
        return pltpu.make_async_remote_copy(
            src_ref=msg2.at[0], dst_ref=recv2.at[grp], send_sem=s2_send.at[peer], recv_sem=s2_recv.at[grp],
            device_id={"grp": peer}, device_id_type=MESH)

    @pl.loop(1, n_grp)
    def _(i):
        copy2(i).start()

    earlier = (iota((n_blk, n_blk), 1) < iota((n_blk, n_blk), 0)).astype(F32).astype(BF16)
    total32 = table[:, VARS:VARS + 1]
    firsts = nn(earlier, table.astype(BF16))[:, VARS:VARS + 1].astype(jnp.int32)
    totals = total32.astype(jnp.int32)
    mine = iota((n_blk, 1), 0) == blk
    first = jnp.sum(jnp.where(mine, firsts, 0))

    q = iota((1, n_blk * SENT_ROWS), 1)
    wanted = lax.rem(q // SENT_ROWS + n_blk * MAXP * pairs - first, n_blk) + n_blk * (q % SENT_ROWS)
    move = (number == wanted).astype(F32).astype(BF16)
    moved = tn(move, entry[...]).astype(BF16).reshape(n_blk, SENT_ROWS, LANES)
    send_rows[...] = moved

    def copy3(i):
        peer = lax.rem(blk + i, n_blk)
        return pltpu.make_async_remote_copy(
            src_ref=send_rows.at[peer], dst_ref=recv_rows.at[blk], send_sem=s3_send.at[peer], recv_sem=s3_recv.at[blk],
            device_id={"blk": peer}, device_id_type=MESH)

    @pl.loop(1, n_blk)
    def _(i):
        copy3(i).start()

    recv_rows[blk] = send_rows[blk]

    skip = lax.rem(blk + n_blk * MAXP * pairs - firsts, n_blk)
    slot0 = (firsts + skip) // n_blk
    live_rows = (totals - skip + n_blk - 1) // n_blk

    def by_row(x):
        return jnp.broadcast_to(x.astype(F32).reshape(n_blk, 1, 1), (n_blk, SENT_ROWS, 1)).reshape(n_blk * SENT_ROWS, 1).astype(jnp.int32)

    k_row = iota((n_blk * SENT_ROWS, 1), 0) % SENT_ROWS
    slot_row = jnp.where(k_row < by_row(live_rows), by_row(slot0) + k_row, -1)
    place_ref[...] = (iota((n_blk * SENT_ROWS, slots), 1) == slot_row).astype(F32).astype(BF16)

    @pl.loop(1, n_grp)
    def _(i):
        peer = lax.rem(grp + i, n_grp)
        pltpu.make_async_remote_copy(
            src_ref=msg2.at[0], dst_ref=recv2.at[peer], send_sem=s2_send.at[peer], recv_sem=s2_recv.at[peer],
            device_id={"grp": peer}, device_id_type=MESH).wait_recv()

    table2 = recv2[...].reshape(n_grp, LANES)
    earlier_groups = jnp.where(iota((n_grp, 1), 0) < grp, table2[:, VARS:VARS + 1], 0.0)
    start_ref[0] = jnp.sum(earlier_groups).astype(jnp.int32) + first
    column_sq = jnp.sum(table2, axis=0, keepdims=True)
    entries = rows * n_grp * n_blk * STATES
    inverse = 1.0 / jnp.sqrt(column_sq / entries + 1e-06)
    inv_ref[...] = jnp.broadcast_to(inverse, (LANES, LANES)).T[:VARS]

    @pl.loop(1, n_blk)
    def _(i):
        peer = lax.rem(blk + i, n_blk)
        pltpu.make_async_remote_copy(
            src_ref=send_rows.at[peer], dst_ref=recv_rows.at[peer], send_sem=s3_send.at[peer], recv_sem=s3_recv.at[peer],
            device_id={"blk": peer}, device_id_type=MESH).wait_recv()

    rows_ref[...] = recv_rows[...]

    @pl.loop(1, n_blk)
    def _(i):
        copy1(i).wait_send()
        copy3(i).wait_send()

    @pl.loop(1, n_grp)
    def _(i):
        copy2(i).wait_send()


def back(defect_ref, inv_ref, place_ref, rows_ref, first_ref, tangent_ref, path_ref, start_ref):
    g = pl.program_id(0)

    @pl.when(g == 0)
    def _():
        start_ref[0] = first_ref[0]
        received = rows_ref[...].reshape(rows_ref.shape[0] * rows_ref.shape[1], LANES)
        path_ref[...] = tn(received, place_ref[...])[:VARS].astype(BF16)

    rows = defect_ref.shape[2]
    inv = jnp.concatenate([inv_ref[...]] * (rows // LANES), axis=1)
    block = (defect_ref[pl.ds(g * GROUP, GROUP)] * inv[None]).astype(BF16)
    tangent_ref[...] = block.reshape(GROUP * VARS, rows).T


def local(n_grp, n_blk, node_vars, w_in, w_out, linear_part, step_len, path_count, path_node, path_con):
    rows = node_vars.shape[1]
    slots = path_count.shape[0] * path_count.shape[1] * MAXP
    vmem = pl.BlockSpec(memory_space=pltpu.VMEM)
    smem = pl.BlockSpec(memory_space=pltpu.SMEM)
    dma = pltpu.SemaphoreType.DMA
    defect, inv, place, received, first = pl.pallas_call(
        functools.partial(front, n_grp, n_blk),
        out_shape=(
            pltpu.VMEM((STATES, VARS, rows), F32),
            pltpu.VMEM((VARS, LANES), F32),
            pltpu.VMEM((n_blk * SENT_ROWS, slots), BF16),
            pltpu.VMEM((n_blk, SENT_ROWS, LANES), BF16),
            jax.ShapeDtypeStruct((1,), jnp.int32),
        ),
        in_specs=[vmem, vmem, vmem, vmem, smem, smem, vmem, vmem],
        out_specs=(vmem, vmem, vmem, vmem, smem),
        scratch_shapes=[
            pltpu.VMEM((UNITS, rows), F32),
            pltpu.VMEM((STEPS, UNITS, GROUP), F32),
            pltpu.VMEM((STEPS, VARS, GROUP), F32),
            pltpu.VMEM((1, rows), F32),
            pltpu.VMEM((slots, LANES), BF16),
            pltpu.VMEM((1, 1, LANES), F32),
            pltpu.VMEM((n_blk, 1, LANES), F32),
            pltpu.VMEM((1, 1, LANES), F32),
            pltpu.VMEM((n_grp, 1, LANES), F32),
            pltpu.VMEM((n_blk, SENT_ROWS, LANES), BF16),
            pltpu.VMEM((n_blk, SENT_ROWS, LANES), BF16),
            dma((n_blk,)), dma((n_blk,)), dma((n_grp,)), dma((n_grp,)), dma((n_blk,)), dma((n_blk,)),
        ],
        compiler_params=pltpu.CompilerParams(collective_id=0, has_side_effects=True, vmem_limit_bytes=40 * 2**20),
        name="front",
    )(node_vars, w_in.T, w_out, linear_part, step_len, path_count, path_node, path_con)
    return pl.pallas_call(
        back,
        grid=(STEPS,),
        out_shape=(
            jax.ShapeDtypeStruct((rows, STATES * VARS), BF16),
            jax.ShapeDtypeStruct((VARS, slots), BF16),
            jax.ShapeDtypeStruct((1,), jnp.int32),
        ),
        in_specs=[vmem, vmem, vmem, vmem, smem],
        out_specs=(
            pl.BlockSpec((rows, GROUP * VARS), lambda g: (0, g)),
            pl.BlockSpec((VARS, slots), lambda g: (0, 0)),
            smem,
        ),
        compiler_params=pltpu.CompilerParams(vmem_limit_bytes=16 * 2**20),
        name="back",
    )(defect, inv, place, received, first)


def solution(mesh):
    both = ("grp", "blk")
    return jax.shard_map(
        functools.partial(local, mesh.shape["grp"], mesh.shape["blk"]),
        mesh=mesh,
        in_specs=(
            P(None, both),
            P(),
            P(),
            P(),
            P(both, None),
            P(both, None),
            P(both, None, None),
            P(both, None, None),
        ),
        out_specs=(P(both, None), P(None, both), P(both)),
        check_vma=False,
    )
```

time: 206 us -> 39.6 us (0.19)
  blocking collectives: 74.2 us -> 0 us
  local copies, waits for them, and re-layouts: 53.6 us -> 0 us
  Pallas kernels: 0 us -> 38.8 us
  matrix products: 31.4 us -> 0 us
  other arithmetic: 24.8 us -> 0 us
  between operations: 16.2 us -> 0.64 us
  starting transfers between devices: 4.13 us -> 0 us
    psum x4 -> x0, blocking collectives: 39 us -> none  [over_axes(): return functools.reduce(lax.psum, axes, shard)]
    pallas_call x0 -> x2, Pallas kernels: none -> 38.8 us  [the longest x1 31.2 us: local(): pl.pallas_call(functools.partial(front, n_grp, n_blk), out_shape=(pltpu.V...]
    unnamed x4 -> x0, blocking collectives: 35.1 us -> none
    dot_general x18 -> x0, matrix products: 31.4 us -> none  [the longest x16 29.1 us: node_blocks(): jnp.dot(scaled.reshape(node_count * STATES, UNITS), w_in, preferred_eleme...]
    reshape x3 -> x0, local copies, waits for them, and re-layouts: 22.7 us -> none  [the longest x1 21.1 us: local(): lax.map(compute_block, slopes_t.reshape(pair_count, NODES, UNITS))]
    scatter x2 -> x0, local copies, waits for them, and re-layouts: 15.4 us -> none  [local(): buffer = jnp.zeros((blk_size, VARS, slot_count), jnp.bfloat16).at[owners,...]
    reduce_sum x3 -> x0, other arithmetic: 13.5 us -> none  [the longest x1 11.3 us: local(): column_sq = over_axes(jnp.sum(defect * defect, axis=(0, 1)), GRP_BLK)]
    convert_element_type x3 -> x0, other arithmetic: 10.9 us -> none  [the longest x1 9.24 us: local(): (defect / column_norm[None, None, :]).astype(jnp.bfloat16)]
  transfers between devices with their start and end apart: 1 -> 0, of which waited for: 0 -> 0; matrix products, arithmetic and copies ran while one was open for 37% -> 0% of each run, Pallas kernels for 0% -> 0%
where the time goes in v1:
time: 39.6 us; the launch traced here: 39.4 us
  Pallas kernels  38.8 us (98%)
  between operations  0.64 us (2%)
    pallas_call x1, Pallas kernels, local(): pl.pallas_call(functools.partial(front, n_grp, n_blk), out_shape=(pltpu.V...  31.2 us
    pallas_call x1, Pallas kernels, local(): pl.pallas_call(back, grid=(STEPS,), out_shape=(jax.ShapeDtypeStruct((rows...  7.59 us

profile of v1, /device:TPU:8, one launch (start us, length us, event | category | flops | bytes accessed | tf_op | source)
XLA Modules:
  0.0 39.4 jit_solution(2773297648050407100)
XLA Ops:
  0.6 31.2 %front.1 = (f32[96,112,384]{2,1,0:T(8,128)S(1)}, f32[112,128]{1,0:T(8,128)S(1)}, bf16[256,256]{1,0:T(8,128)(2,1)S(1)}, bf16[32,8,128]{2,1,0:T(8,128)(2,1)S(1)}, s32[1]{0:T(128)}) custom-call(bf16[112,384]{1,0:T(8,128)(2,1)} %vars_ref.1, bf16[112,512]{1,0:T(8,128)(2,1)} %bitcast.1, bf16[96,512]{1,0:T(8,128)(2,1)} %w_out_ref.1, bf16[96,112]{1,0:T(8,128)(2,1)} %linear_ref.1, ...), custom_call_target="tpu_custom_call" | custom-call | tf_op jit(solution)/shard_map/front/pallas_call | solution.py:290
  31.8 7.6 %back.1 = (bf16[384,10752]{1,0:T(8,128)(2,1)}, bf16[112,256]{1,0:T(8,128)(2,1)}, s32[1]{0:T(128)}) custom-call(f32[96,112,384]{2,1,0:T(8,128)S(1)} %get-tuple-element.8.defect_ref, f32[112,128]{1,0:T(8,128)S(1)} %get-tuple-element.9.inv_ref, bf16[256,256]{1,0:T(8,128)(2,1)S(1)} %get-tuple-element.10.place_ref, ...), custom_call_target="tpu_custom_call" | custom-call | tf_op jit(solution)/shard_map/back/pallas_call | solution.py:318

commit v2 on v1

--- a/solution.py
+++ b/solution.py
@@ -16,7 +16,8 @@
 GROUP = 8
 STEPS = STATES // GROUP
 SENT_ROWS = 8
-EARLY = 2
+FIRST = 7
+WRITES = 8
 MESH = pl.DeviceIdType.MESH
 BF16 = jnp.bfloat16
 F32 = jnp.float32
@@ -56,9 +57,10 @@
 
 def front(
     n_grp, n_blk,
-    vars_ref, w_in_t_ref, w_out_ref, linear_ref, step_ref, count_ref, node_ref, con_ref,
-    defect_ref, inv_ref, place_ref, rows_ref, start_ref,
-    slopes, w_cols, l_cols, half_row, entry, msg1, recv1, msg2, recv2, send_rows, recv_rows,
+    vars_any, w_in_t_any, w_out_any, linear_any, step_any, count_any, node_any, con_any,
+    tangent_ref, path_ref, start_ref,
+    vars_ref, w_in_t_ref, w_out_ref, linear_ref, step_ref, count_ref, node_ref, con_ref, in_sem,
+    defect_ref, slopes, w_cols, l_cols, half_row, entry, msg1, recv1, msg2, recv2, send_rows, recv_rows,
     s1_send, s1_recv, s2_send, s2_recv, s3_send, s3_recv,
 ):
     grp, blk = lax.axis_index("grp"), lax.axis_index("blk")
@@ -67,6 +69,12 @@
     rows = vars_ref.shape[1]
     slots = pairs * MAXP
 
+    sources = (vars_any, w_in_t_any, w_out_any, linear_any, step_any, count_any, node_any, con_any)
+    targets = (vars_ref, w_in_t_ref, w_out_ref, linear_ref, step_ref, count_ref, node_ref, con_ref)
+    loads = [pltpu.make_async_copy(a, b, in_sem.at[i]) for i, (a, b) in enumerate(zip(sources, targets))]
+    for load in loads:
+        load.start()
+
     barrier = pltpu.get_barrier_semaphore()
 
     @pl.loop(1, n_blk)
@@ -76,6 +84,9 @@
     @pl.loop(1, n_grp)
     def _(i):
         pl.semaphore_signal(barrier, inc=1, device_id={"grp": lax.rem(grp + i, n_grp)}, device_id_type=MESH)
+
+    for load in loads:
+        load.wait()
 
     w_in_t = w_in_t_ref[...]
     w_out = w_out_ref[...]
@@ -112,6 +123,18 @@
     msg1[0] = message
     recv1[blk] = message
 
+    pl.semaphore_wait(barrier, n_blk + n_grp - 2)
+
+    def copy1(i):
+        peer = lax.rem(blk + i, n_blk)
+        return pltpu.make_async_remote_copy(
+            src_ref=msg1.at[0], dst_ref=recv1.at[blk], send_sem=s1_send.at[peer], recv_sem=s1_recv.at[blk],
+            device_id={"blk": peer}, device_id_type=MESH)
+
+    @pl.loop(1, n_blk)
+    def _(i):
+        copy1(i).start()
+
     w_t = w_out.astype(F32).T
     l_t = linear32.T
     for g in range(STEPS):
@@ -154,23 +177,7 @@
     entry_rows = nt(scaled_rows, w_in_t) + nn(pick_con, linear)
     entry[...] = jnp.concatenate([entry_rows, jnp.zeros((slots, LANES - VARS), F32)], axis=1).astype(BF16)
 
-    @pl.loop(0, EARLY)
-    def _(g):
-        main(g)
-
-    pl.semaphore_wait(barrier, n_blk + n_grp - 2)
-
-    def copy1(i):
-        peer = lax.rem(blk + i, n_blk)
-        return pltpu.make_async_remote_copy(
-            src_ref=msg1.at[0], dst_ref=recv1.at[blk], send_sem=s1_send.at[peer], recv_sem=s1_recv.at[blk],
-            device_id={"blk": peer}, device_id_type=MESH)
-
-    @pl.loop(1, n_blk)
-    def _(i):
-        copy1(i).start()
-
-    @pl.loop(EARLY, STEPS)
+    @pl.loop(0, FIRST)
     def _(g):
         main(g)
 
@@ -230,7 +237,11 @@
 
     k_row = iota((n_blk * SENT_ROWS, 1), 0) % SENT_ROWS
     slot_row = jnp.where(k_row < by_row(live_rows), by_row(slot0) + k_row, -1)
-    place_ref[...] = (iota((n_blk * SENT_ROWS, slots), 1) == slot_row).astype(F32).astype(BF16)
+    place = (iota((n_blk * SENT_ROWS, slots), 1) == slot_row).astype(F32).astype(BF16)
+
+    @pl.loop(FIRST, STEPS)
+    def _(g):
+        main(g)
 
     @pl.loop(1, n_grp)
     def _(i):
@@ -241,11 +252,16 @@
 
     table2 = recv2[...].reshape(n_grp, LANES)
     earlier_groups = jnp.where(iota((n_grp, 1), 0) < grp, table2[:, VARS:VARS + 1], 0.0)
-    start_ref[0] = jnp.sum(earlier_groups).astype(jnp.int32) + first
+    start_ref[...] = jnp.full(start_ref.shape, jnp.sum(earlier_groups).astype(jnp.int32) + first)
     column_sq = jnp.sum(table2, axis=0, keepdims=True)
     entries = rows * n_grp * n_blk * STATES
     inverse = 1.0 / jnp.sqrt(column_sq / entries + 1e-06)
-    inv_ref[...] = jnp.broadcast_to(inverse, (LANES, LANES)).T[:VARS]
+    inv = jnp.broadcast_to(inverse, (LANES, LANES)).T[:VARS]
+    inv = jnp.concatenate([inv] * (rows // LANES), axis=1)
+
+    for g in range(STEPS):
+        block = (defect_ref[pl.ds(g * GROUP, GROUP)] * inv[None]).astype(BF16)
+        tangent_ref[:, g * GROUP * VARS:(g + 1) * GROUP * VARS] = block.reshape(GROUP * VARS, rows).T
 
     @pl.loop(1, n_blk)
     def _(i):
@@ -254,7 +270,8 @@
             src_ref=send_rows.at[peer], dst_ref=recv_rows.at[peer], send_sem=s3_send.at[peer], recv_sem=s3_recv.at[peer],
             device_id={"blk": peer}, device_id_type=MESH).wait_recv()
 
-    rows_ref[...] = recv_rows[...]
+    received = recv_rows[...].reshape(n_blk * SENT_ROWS, LANES)
+    path_ref[...] = tn(received, place)[:VARS].astype(BF16)
 
     @pl.loop(1, n_blk)
     def _(i):
@@ -266,39 +283,40 @@
         copy2(i).wait_send()
 
 
-def back(defect_ref, inv_ref, place_ref, rows_ref, first_ref, tangent_ref, path_ref, start_ref):
-    g = pl.program_id(0)
-
-    @pl.when(g == 0)
-    def _():
-        start_ref[0] = first_ref[0]
-        received = rows_ref[...].reshape(rows_ref.shape[0] * rows_ref.shape[1], LANES)
-        path_ref[...] = tn(received, place_ref[...])[:VARS].astype(BF16)
-
-    rows = defect_ref.shape[2]
-    inv = jnp.concatenate([inv_ref[...]] * (rows // LANES), axis=1)
-    block = (defect_ref[pl.ds(g * GROUP, GROUP)] * inv[None]).astype(BF16)
-    tangent_ref[...] = block.reshape(GROUP * VARS, rows).T
+def back(tangent_ref, path_ref, start_ref, tangent_any, path_any, start_any, first, sem):
+    first[...] = jnp.full((1,), jnp.max(start_ref[...]))
+    rows = tangent_ref.shape[0] // WRITES
+    copies = [pltpu.make_async_copy(first, start_any, sem.at[WRITES + 1]), pltpu.make_async_copy(path_ref, path_any, sem.at[WRITES])]
+    for i in range(WRITES):
+        part = pl.ds(i * rows, rows)
+        copies.append(pltpu.make_async_copy(tangent_ref.at[part], tangent_any.at[part], sem.at[i]))
+    for copy in copies:
+        copy.start()
+    for copy in copies:
+        copy.wait()
 
 
 def local(n_grp, n_blk, node_vars, w_in, w_out, linear_part, step_len, path_count, path_node, path_con):
     rows = node_vars.shape[1]
     slots = path_count.shape[0] * path_count.shape[1] * MAXP
     vmem = pl.BlockSpec(memory_space=pltpu.VMEM)
-    smem = pl.BlockSpec(memory_space=pltpu.SMEM)
     dma = pltpu.SemaphoreType.DMA
-    defect, inv, place, received, first = pl.pallas_call(
+    hbm = pl.BlockSpec(memory_space=pl.ANY)
+    operands = (node_vars, w_in.T, w_out, linear_part, step_len, path_count, path_node, path_con)
+    scalars = (4, 5)
+    homes = [(pltpu.SMEM if i in scalars else pltpu.VMEM)(x.shape, x.dtype) for i, x in enumerate(operands)]
+    done = pl.pallas_call(
         functools.partial(front, n_grp, n_blk),
         out_shape=(
+            pltpu.VMEM((rows, STATES * VARS), BF16),
+            pltpu.VMEM((VARS, slots), BF16),
+            pltpu.VMEM((8, LANES), jnp.int32),
+        ),
+        in_specs=[hbm] * len(operands),
+        out_specs=(vmem, vmem, vmem),
+        scratch_shapes=homes + [
+            dma((len(operands),)),
             pltpu.VMEM((STATES, VARS, rows), F32),
-            pltpu.VMEM((VARS, LANES), F32),
-            pltpu.VMEM((n_blk * SENT_ROWS, slots), BF16),
-            pltpu.VMEM((n_blk, SENT_ROWS, LANES), BF16),
-            jax.ShapeDtypeStruct((1,), jnp.int32),
-        ),
-        in_specs=[vmem, vmem, vmem, vmem, smem, smem, vmem, vmem],
-        out_specs=(vmem, vmem, vmem, vmem, smem),
-        scratch_shapes=[
             pltpu.VMEM((UNITS, rows), F32),
             pltpu.VMEM((STEPS, UNITS, GROUP), F32),
             pltpu.VMEM((STEPS, VARS, GROUP), F32),
@@ -312,26 +330,22 @@
             pltpu.VMEM((n_blk, SENT_ROWS, LANES), BF16),
             dma((n_blk,)), dma((n_blk,)), dma((n_grp,)), dma((n_grp,)), dma((n_blk,)), dma((n_blk,)),
         ],
-        compiler_params=pltpu.CompilerParams(collective_id=0, has_side_effects=True, vmem_limit_bytes=40 * 2**20),
+        compiler_params=pltpu.CompilerParams(collective_id=0, has_side_effects=True, vmem_limit_bytes=50 * 2**20),
         name="front",
-    )(node_vars, w_in.T, w_out, linear_part, step_len, path_count, path_node, path_con)
+    )(*operands)
     return pl.pallas_call(
         back,
-        grid=(STEPS,),
         out_shape=(
             jax.ShapeDtypeStruct((rows, STATES * VARS), BF16),
             jax.ShapeDtypeStruct((VARS, slots), BF16),
             jax.ShapeDtypeStruct((1,), jnp.int32),
         ),
-        in_specs=[vmem, vmem, vmem, vmem, smem],
-        out_specs=(
-            pl.BlockSpec((rows, GROUP * VARS), lambda g: (0, g)),
-            pl.BlockSpec((VARS, slots), lambda g: (0, 0)),
-            smem,
-        ),
-        compiler_params=pltpu.CompilerParams(vmem_limit_bytes=16 * 2**20),
+        in_specs=[vmem] * 3,
+        out_specs=(hbm, hbm, hbm),
+        scratch_shapes=[pltpu.VMEM((1,), jnp.int32), dma((WRITES + 2,))],
+        compiler_params=pltpu.CompilerParams(vmem_limit_bytes=2**20),
         name="back",
-    )(defect, inv, place, received, first)
+    )(*done)
 
 
 def solution(mesh):

time: 39.6 us -> 35.2 us (0.89); the launches traced: 39.4 us -> 34.6 us
  Pallas kernels: 38.8 us -> 33.9 us
    pallas_call x1, Pallas kernels: 7.59 us -> 3.59 us  [local(): pl.pallas_call(back, out_shape=(jax.ShapeDtypeStruct((rows, STATES * VARS...]
    pallas_call x1, Pallas kernels: 31.2 us -> 30.3 us  [local(): pl.pallas_call(functools.partial(front, n_grp, n_blk), out_shape=(pltpu.V...]
where the time goes in v2:
time: 35.2 us; the launch traced here: 34.6 us
  Pallas kernels  33.9 us (96%)
  between operations  0.64 us (2%)
    pallas_call x1, Pallas kernels, local(): pl.pallas_call(functools.partial(front, n_grp, n_blk), out_shape=(pltpu.V...  30.3 us
    pallas_call x1, Pallas kernels, local(): pl.pallas_call(back, out_shape=(jax.ShapeDtypeStruct((rows, STATES * VARS...  3.59 us

profile of v2, /device:TPU:8, one launch (start us, length us, event | category | flops | bytes accessed | tf_op | source)
XLA Modules:
  0.0 34.6 jit_solution(12071418867199483541)
XLA Ops:
  0.6 30.3 %front.1 = (bf16[384,10752]{1,0:T(8,128)(2,1)S(1)}, bf16[112,256]{1,0:T(8,128)(2,1)S(1)}, s32[8,128]{1,0:T(8,128)S(1)}) custom-call(bf16[112,384]{1,0:T(8,128)(2,1)} %vars_any.1, bf16[112,512]{1,0:T(8,128)(2,1)} %bitcast.1, bf16[96,512]{1,0:T(8,128)(2,1)} %w_out_any.1, bf16[96,112]{1,0:T(8,128)(2,1)} %linear_any.1, f32[2,8]{1,0:T(2,128)} %step_any.1, ...), custom_call_target="tpu_custom_call" | custom-call | tf_op jit(solution)/shard_map/front/pallas_call | solution.py:308
  31.0 3.6 %back.1 = (bf16[384,10752]{1,0:T(8,128)(2,1)}, bf16[112,256]{1,0:T(8,128)(2,1)}, s32[1]{0:T(128)}) custom-call(bf16[384,10752]{1,0:T(8,128)(2,1)S(1)} %get-tuple-element.6.tangent_ref, bf16[112,256]{1,0:T(8,128)(2,1)S(1)} %get-tuple-element.7.path_ref, s32[8,128]{1,0:T(8,128)S(1)} %get-tuple-element.8.start_ref), custom_call_target="tpu_custom_call" | custom-call | tf_op jit(solution)/shard_map/back/pallas_call | solution.py:336
